TPU v7x, 32 devices: a whole 2x2x4 slice. The times are simulated.
32 devices in a mesh: gx: 4 (over y, x), gy: 8 (over z, core).
Axes of the slice: x: 2, y: 2, z: 4, core: 2. Of those that a mesh axis runs over, the one named last changes fastest.
Arguments:
- pressure: float32 [96, 192, 256], P('gx', 'gy'), may hold values from -6 to 6
- pressure_old: float32 [96, 192, 256], P('gx', 'gy'), may hold values from -6 to 6
- speed_term: float32 [96, 192, 256], P('gx', 'gy'), may hold values from 0.03 to 0.15
- layer_width: int32 [4], replicated, may hold values from 8 to 16
- source_x: int32 [4], replicated, may hold values from 0 to 95
- source_y: int32 [4], replicated, may hold values from 0 to 191
- source_z: int32 [4], replicated, may hold values from 0 to 255
- source_amp: float32 [8, 4], replicated, may hold values from -8 to 8
- receiver_x: int32 [64], replicated, may hold values from 0 to 95
- receiver_y: int32 [64], replicated, may hold values from 0 to 191
- receiver_z: int32 [64], replicated, may hold values from 0 to 255
Outputs:
- pressure_final: float32 [96, 192, 256], P('gx', 'gy')
- traces: float32 [64, 8], replicated
- energy: float32 [8], replicated
All inputs are finite; a program needn't handle non-finite values.
Results may differ from a plain program's by a relative error of at most 0.00026.
Values sent between devices are 32-bit elements; how exact they have to be, the bound alone decides.
A program may use at most 64 MiB of HBM per device.

v0:
```python
import functools

import jax
import jax.numpy as jnp
from jax import lax
from jax.experimental import pallas as pl
from jax.experimental.pallas import tpu as pltpu
from jax.sharding import PartitionSpec as P

MESH = pl.DeviceIdType.MESH
F32 = jnp.float32
BF16 = jnp.bfloat16
first_coef = (0.8, -0.2, 4.0 / 105.0, -1.0 / 280.0)
second_coef = (1.6, -0.2, 8.0 / 315.0, -1.0 / 560.0)
centre_coef = -205.0 / 72.0
damping = 0.6
radius = 4
GROUP = 8


def split(value):
    high = value.astype(BF16)
    low = (value - high.astype(F32)).astype(BF16)
    return high, low


def dot(a, b):
    return jnp.dot(a, b, preferred_element_type=F32)


def by_distance(distance, coefs, centre):
    out = jnp.where(distance == 0, centre, 0.0)
    for k in range(1, 5):
        out = jnp.where(distance == k, coefs[k - 1], out)
    return out


def profile(position, low_width, high_width, length):
    inward_low = jnp.clip((low_width - position) / low_width, 0.0, 1.0)
    inward_high = jnp.clip((position - (length - 1 - high_width)) / high_width, 0.0, 1.0)
    return jnp.exp(-damping * (inward_low * inward_low + inward_high * inward_high))


def iota(shape, dim):
    return lax.broadcasted_iota(jnp.int32, shape, dim)


def kernel(
    ngx, ngy,
    pressure, pressure_old, speed, widths_in, sx_in, sy_in, sz_in, amp_in, rx_in, ry_in, rz_in,
    out, out_traces, out_energy,
    F, SP, LAP, FH, FL, HX, HY, MX, ZX, MY, ZY,
    BZ, BY, DY, R32, RB, ZM, PS, KX, KY, W, TR, TE, R1, R2,
    widths, src_x, src_y, src_z, amp, rec_x, rec_y, rec_z, small_sem, load_sem, send_sem, recv_sem, r1_send, r1_recv, r2_send, r2_recv,
):
    cx, cy, nz = pressure.shape
    nsrc, steps = amp.shape
    nrec = rec_x.shape[0]
    gx, gy = lax.axis_index("gx"), lax.axis_index("gy")
    x0, y0 = gx * cx, gy * cy
    count_x, count_y = ngx * cx, ngy * cy
    groups = cx // GROUP
    grows = GROUP * cy

    loads = [
        pltpu.make_async_copy(pressure, F.at[0, pl.ds(radius, cx)], load_sem.at[0]),
        pltpu.make_async_copy(pressure_old, F.at[1, pl.ds(radius, cx)], load_sem.at[1]),
        pltpu.make_async_copy(speed, SP, load_sem.at[2]),
    ]
    smalls = [
        pltpu.make_async_copy(src, dst, small_sem.at[n])
        for n, (src, dst) in enumerate((
            (widths_in, widths), (sx_in, src_x), (sy_in, src_y), (sz_in, src_z),
            (amp_in, amp), (rx_in, rec_x), (ry_in, rec_y), (rz_in, rec_z),
        ))
    ]
    for load in loads + smalls:
        load.start()

    HX[...] = jnp.zeros_like(HX)
    HY[...] = jnp.zeros_like(HY)

    barrier = pltpu.get_barrier_semaphore()
    for o in range(1, ngx):
        pl.semaphore_signal(barrier, inc=1, device_id={"gx": lax.rem(gx + o, ngx)}, device_id_type=MESH)
    for o in range(1, ngy):
        pl.semaphore_signal(barrier, inc=1, device_id={"gy": lax.rem(gy + o, ngy)}, device_id_type=MESH)
    pl.semaphore_wait(barrier, ngx - 1 + ngy - 1)

    def halos(s):
        f = F.at[s]

        def send(k, src, dst, target):
            return pltpu.make_async_remote_copy(
                src_ref=src, dst_ref=dst, send_sem=send_sem.at[k], recv_sem=recv_sem.at[s, k],
                device_id=target, device_id_type=MESH,
            )

        return (
            (gx < ngx - 1, gx > 0, send(0, f.at[pl.ds(cx, radius)], HX.at[s, 0], {"gx": gx + 1})),
            (gx > 0, gx < ngx - 1, send(1, f.at[pl.ds(radius, radius)], HX.at[s, 1], {"gx": gx - 1})),
            (gy < ngy - 1, gy > 0, send(2, f.at[pl.ds(radius, cx), pl.ds(cy - radius, radius)],
                                        HY.at[s, :, pl.ds(0, radius)], {"gy": gy + 1})),
            (gy > 0, gy < ngy - 1, send(3, f.at[pl.ds(radius, cx), pl.ds(0, radius)],
                                        HY.at[s, :, pl.ds(radius, radius)], {"gy": gy - 1})),
        )

    upper_first = lax.rem(gx, 2) == 1

    def start_sends(s):
        h = halos(s)

        def go(k):
            @pl.when(h[k][0])
            def _():
                h[k][2].start()

        @pl.when(upper_first)
        def _():
            go(0)
            go(1)

        @pl.when(jnp.logical_not(upper_first))
        def _():
            go(1)
            go(0)

        go(2)
        go(3)

    loads[0].wait()
    start_sends(0)

    for s in range(2):
        F[s, 0:radius] = jnp.zeros((radius, cy, nz), F32)
        F[s, cx + radius:cx + 2 * radius] = jnp.zeros((radius, cy, nz), F32)
        MX[s] = jnp.zeros(MX.shape[1:], F32)
    ZX[...] = jnp.zeros_like(ZX)
    MY[...] = jnp.zeros_like(MY)
    ZY[...] = jnp.zeros_like(ZY)
    TR[...] = jnp.zeros_like(TR)
    TE[...] = jnp.zeros_like(TE)

    z_diff = iota((nz, nz), 0) - iota((nz, nz), 1)
    BZ[0], BZ[1] = split(by_distance(jnp.abs(z_diff), second_coef, centre_coef))

    def block_of(index, size):
        return jnp.floor((index.astype(F32) + 0.5) * (1.0 / size)).astype(jnp.int32)

    row, col = iota((grows, grows), 0), iota((grows, grows), 1)
    same = block_of(row, cy) == block_of(col, cy)
    diff = col - row
    BY[0], BY[1] = split(jnp.where(same, by_distance(jnp.abs(diff), second_coef, centre_coef), 0.0))
    signed = by_distance(jnp.abs(diff), first_coef, 0.0)
    DY[0], DY[1] = split(jnp.where(same, jnp.where(diff > 0, signed, -signed), 0.0))
    for load in smalls:
        load.wait()
    w = [widths[i].astype(F32) for i in range(4)]
    KX[...] = profile((iota(KX.shape, 0) + x0).astype(F32), w[0], w[1], count_x)
    KY[...] = profile((iota(KY.shape, 0) + y0).astype(F32), w[2], w[3], count_y)
    for i in range(cx):
        W[i] = 1.0 - KX[i, 0:1] * KY[...]
    yy, zz = iota((cy, nz), 0) + y0, iota((cy, nz), 1)
    for s in range(nsrc):
        PS[s] = jnp.where((yy == src_y[s]) & (zz == src_z[s]), 1.0, 0.0)

    cells = iota((1, cx * cy), 1)
    lanes = iota((1, nz), 1)

    def one_receiver(r, carry):
        lx, ly = rec_x[r] - x0, rec_y[r] - y0
        owned = (lx >= 0) & (lx < cx) & (ly >= 0) & (ly < cy)
        cell = jnp.where(owned, lx * cy + ly, -1)
        R32[pl.ds(r, 1), :] = jnp.where(cells == cell, 1.0, 0.0)
        ZM[pl.ds(r, 1), :] = jnp.where(lanes == rec_z[r], 1.0, 0.0)
        return carry

    lax.fori_loop(0, nrec, one_receiver, 0)
    RB[...] = R32[...].astype(BF16)
    loads[1].wait()
    loads[2].wait()

    edge_x = (gx == 0) | (gx == ngx - 1)
    edge_y = (gy == 0) | (gy == ngy - 1)
    te_row, te_lane = iota(TE.shape, 0), iota(TE.shape, 1)
    tr_lane = iota(TR.shape, 1)

    def split_group(s, g):
        rows = pl.ds(g * grows, grows)
        fh, fl = split(F[s, pl.ds(radius + g * GROUP, GROUP)].reshape(grows, nz))
        FH[rows, :], FL[rows, :] = fh, fl
        return fh, fl

    def record(t, e):
        total = jnp.sum(jnp.sum(e, axis=0, keepdims=True), axis=1, keepdims=True)
        TE[...] = jnp.where((te_row == t) & (te_lane == nrec), total, TE[...])
        g = (dot(RB[...], FH[...]) + dot(RB[...], FL[...])) * ZM[...]
        TR[...] = jnp.where(tr_lane == t, jnp.sum(g, axis=1, keepdims=True), TR[...])

    p8 = iota((8, nz), 0)
    up, down = [], []
    for d in range(radius):
        c = second_coef[radius - 1 - d]
        up.append(jnp.where(p8 + d < radius, c, 0.0))
        down.append(jnp.where(p8 - d >= radius, c, 0.0))

    def step(t, carry):
        s = lax.rem(t, 2)
        o = 1 - s


        for g in range(groups):
            xs = pl.ds(g * GROUP, GROUP)
            fh, fl = split_group(s, g)
            sz = dot(fh, BZ[0]) + dot(fl, BZ[0]) + dot(fh, BZ[1])
            sy = dot(BY[0], fh) + dot(BY[0], fl) + dot(BY[1], fh)

            @pl.when(jnp.logical_not(edge_y))
            def _():
                LAP[xs] = (sz + sy).reshape(GROUP, cy, nz)

            @pl.when(edge_y)
            def _():
                ky = KY[...][None]
                ty = ky - 1.0
                mh, ml = split(MY[xs].reshape(grows, nz))
                dm = dot(DY[0], mh) + dot(DY[0], ml) + dot(DY[1], mh)
                bend = (sy + dm).reshape(GROUP, cy, nz)
                zy = ky * ZY[xs] + ty * bend
                ZY[xs] = zy
                LAP[xs] = sz.reshape(GROUP, cy, nz) + bend + zy
                df = dot(DY[0], fh) + dot(DY[0], fl) + dot(DY[1], fh)
                MY[xs] = ky * MY[xs] + ty * df.reshape(GROUP, cy, nz)

        def second_x(i):
            v = centre_coef * F[s, radius + i]
            for k in range(1, 5):
                v += second_coef[k - 1] * (F[s, radius + i + k] + F[s, radius + i - k])
            return v

        def first(ref, i):
            v = first_coef[0] * (ref[s, radius + i + 1] - ref[s, radius + i - 1])
            for k in range(2, 5):
                v += first_coef[k - 1] * (ref[s, radius + i + k] - ref[s, radius + i - k])
            return v

        def update(edge, i, e):
            f = F[s, radius + i]
            bend = second_x(i)
            lap = LAP[i]
            if edge:
                kx = KX[i, 0:1]
                tx = kx - 1.0
                bend += first(MX, i)
                zx = kx * ZX[i] + tx * bend
                ZX[i] = zx
                lap += zx
                MX[o, radius + i] = kx * MX[s, radius + i] + tx * first(F, i)
            v = 2.0 * f - F[o, radius + i] + SP[i] * (lap + bend)
            for q in range(nsrc):
                v += jnp.where(src_x[q] - x0 == i, amp[q, t], 0.0) * PS[q]
            F[o, radius + i] = v
            return e + W[i] * (f * f)

        def finish(edge):
            record(t - 1, lax.fori_loop(0, cx, functools.partial(update, edge), jnp.zeros((cy, nz), F32)))

        @pl.when(edge_x)
        def _():
            finish(True)

        @pl.when(jnp.logical_not(edge_x))
        def _():
            finish(False)

        now, later = halos(s), halos(o)
        more = t < steps - 1

        def received(k):
            @pl.when(now[k][1])
            def _():
                now[k][2].wait_recv()

        def resend(k):
            @pl.when(now[k][0])
            def _():
                now[k][2].wait_send()

            @pl.when(now[k][0] & more)
            def _():
                later[k][2].start()

        received(2)
        received(3)

        def halo_y(i, c):
            h = HY[s, i]
            v = (up[0] + down[0]) * h
            for d in range(1, radius):
                v += up[d] * pltpu.roll(h, 8 - d, 0) + down[d] * pltpu.roll(h, d, 0)
            F[o, radius + i, 0:8] += SP[i, 0:8] * jnp.where(p8 < radius, v, 0.0)
            F[o, radius + i, cy - 8:cy] += SP[i, cy - 8:cy] * jnp.where(p8 < radius, 0.0, v)
            return c

        lax.fori_loop(0, cx, halo_y, 0, unroll=4)

        def low_side():
            @pl.when(gx > 0)
            def _():
                now[0][2].wait_recv()
                for j in range(radius):
                    v = second_coef[j] * HX[s, 0, radius - 1]
                    for k in range(j + 2, 5):
                        v += second_coef[k - 1] * HX[s, 0, radius + j - k]
                    F[o, radius + j] += SP[j] * v
            resend(1)

        def high_side():
            @pl.when(gx < ngx - 1)
            def _():
                now[1][2].wait_recv()
                for j in range(radius):
                    i = cx - 1 - j
                    v = second_coef[j] * HX[s, 1, 0]
                    for k in range(j + 2, 5):
                        v += second_coef[k - 1] * HX[s, 1, k - 1 - j]
                    F[o, radius + i] += SP[i] * v
            resend(0)

        @pl.when(upper_first)
        def _():
            high_side()
            low_side()

        @pl.when(jnp.logical_not(upper_first))
        def _():
            low_side()
            high_side()

        resend(2)
        resend(3)
        return carry

    lax.fori_loop(0, steps, step, 0)
    last = steps % 2
    store = pltpu.make_async_copy(F.at[last, pl.ds(radius, cx)], out, load_sem.at[0])
    store.start()
    for g in range(groups):
        split_group(last, g)

    def energy_row(i, e):
        f = F[last, radius + i]
        return e + W[i] * (f * f)

    record(steps - 1, lax.fori_loop(0, cx, energy_row, jnp.zeros((cy, nz), F32)))
    flat = jnp.transpose(TR[...])[0:steps]
    TE[...] += jnp.concatenate([flat, jnp.zeros((steps, TE.shape[1] - nrec), F32)], axis=1)

    def reduce_over(axis, me, n, buf, send, recv):
        buf[me] = TE[...]

        def copy(slot, k, target):
            return pltpu.make_async_remote_copy(
                src_ref=TE, dst_ref=buf.at[slot], send_sem=send.at[k], recv_sem=recv.at[slot],
                device_id={axis: target}, device_id_type=MESH,
            )

        for o in range(1, n):
            copy(me, o, lax.rem(me + o, n)).start()
        for o in range(1, n):
            copy(lax.rem(me + o, n), o, lax.rem(me + o, n)).wait_recv()
        for o in range(1, n):
            copy(me, o, lax.rem(me + o, n)).wait_send()
        v = buf[0]
        for j in range(1, n):
            v += buf[j]
        TE[...] = v

    reduce_over("gx", gx, ngx, R1, r1_send, r1_recv)
    reduce_over("gy", gy, ngy, R2, r2_send, r2_recv)

    def total_of(count, low, high):
        return jnp.sum(profile(iota((1, count), 1).astype(F32), low, high, count), axis=1, keepdims=True)

    norm = nz * (float(count_x * count_y) - total_of(count_x, w[0], w[1]) * total_of(count_y, w[2], w[3]))
    out_traces[...] = TE[:, 0:nrec]
    out_energy[...] = jnp.transpose(TE[...])[nrec:nrec + 1] / norm
    store.wait()


def solution(mesh):
    ngx, ngy = mesh.shape["gx"], mesh.shape["gy"]

    def per_device(pressure, pressure_old, speed, widths, sx, sy, sz, amp, rx, ry, rz):
        cx, cy, nz = pressure.shape
        steps, nsrc = amp.shape
        nrec = rx.shape[0]
        lanes = (nrec // 128 + 1) * 128
        vmem = functools.partial(pltpu.VMEM)
        grows = GROUP * cy
        final, traces, energy = pl.pallas_call(
            functools.partial(kernel, ngx, ngy),
            out_shape=(
                jax.ShapeDtypeStruct((cx, cy, nz), F32),
                jax.ShapeDtypeStruct((steps, nrec), F32),
                jax.ShapeDtypeStruct((1, steps), F32),
            ),
            in_specs=[pl.BlockSpec(memory_space=pltpu.HBM)] * 11,
            out_specs=(
                pl.BlockSpec(memory_space=pl.ANY),
                pl.BlockSpec(memory_space=pltpu.VMEM),
                pl.BlockSpec(memory_space=pltpu.VMEM),
            ),
            scratch_shapes=[
                vmem((2, cx + 2 * radius, cy, nz), F32),
                vmem((cx, cy, nz), F32),
                vmem((cx, cy, nz), F32),
                vmem((cx * cy, nz), BF16),
                vmem((cx * cy, nz), BF16),
                vmem((2, 2, radius, cy, nz), F32),
                vmem((2, cx, 2 * radius, nz), F32),
                vmem((2, cx + 2 * radius, cy, nz), F32),
                vmem((cx, cy, nz), F32),
                vmem((cx, cy, nz), F32),
                vmem((cx, cy, nz), F32),
                vmem((2, nz, nz), BF16),
                vmem((2, grows, grows), BF16),
                vmem((2, grows, grows), BF16),
                vmem((nrec, cx * cy), F32),
                vmem((nrec, cx * cy), BF16),
                vmem((nrec, nz), F32),
                vmem((nsrc, cy, nz), F32),
                vmem((cx, 8, nz), F32),
                vmem((cy, nz), F32),
                vmem((cx, cy, nz), F32),
                vmem((nrec, 128), F32),
                vmem((steps, lanes), F32),
                vmem((ngx, steps, lanes), F32),
                vmem((ngy, steps, lanes), F32),
                pltpu.SMEM(widths.shape, jnp.int32),
                pltpu.SMEM(sx.shape, jnp.int32),
                pltpu.SMEM(sy.shape, jnp.int32),
                pltpu.SMEM(sz.shape, jnp.int32),
                pltpu.SMEM((nsrc, steps), F32),
                pltpu.SMEM(rx.shape, jnp.int32),
                pltpu.SMEM(ry.shape, jnp.int32),
                pltpu.SMEM(rz.shape, jnp.int32),
                pltpu.SemaphoreType.DMA((8,)),
                pltpu.SemaphoreType.DMA((3,)),
                pltpu.SemaphoreType.DMA((4,)),
                pltpu.SemaphoreType.DMA((2, 4)),
                pltpu.SemaphoreType.DMA((ngx,)),
                pltpu.SemaphoreType.DMA((ngx,)),
                pltpu.SemaphoreType.DMA((ngy,)),
                pltpu.SemaphoreType.DMA((ngy,)),
            ],
            compiler_params=pltpu.CompilerParams(
                collective_id=0, has_side_effects=True, vmem_limit_bytes=67043328
            ),
            name="wave",
        )(pressure, pressure_old, speed, widths, sx, sy, sz, amp.T, rx, ry, rz)
        return final, traces.T, energy.reshape(steps)

    in_specs = (P("gx", "gy", None),) * 3 + (P(),) * 8
    out_specs = (P("gx", "gy", None), P(), P())
    return jax.shard_map(per_device, mesh=mesh, in_specs=in_specs, out_specs=out_specs, check_vma=False)
```

profile of v0, /device:TPU:0, one launch (start us, length us, event | category | flops | bytes accessed | tf_op | source)
XLA Modules:
  0.0 55.6 jit_solution(14981583671292387603)
XLA Ops:
  0.6 51.9 %wave.1 = (f32[24,24,256]{2,1,0:T(8,128)}, f32[8,64]{1,0:T(8,128)}, f32[1,8]{1,0:T(1,128)}) custom-call(f32[24,24,256]{2,1,0:T(8,128)} %pressure.1, f32[24,24,256]{2,1,0:T(8,128)} %pressure_old.1, f32[24,24,256]{2,1,0:T(8,128)} %speed.1, s32[4]{0:T(128)} %widths_in.1, s32[4]{0:T(128)} %sx_in.1, s32[4]{0:T(128)} %sy_in.1, s32[4]{0:T(128)} %sz_in.1, ...), custom_call_target="tpu_custom_call" | custom-call | tf_op jit(solution)/shard_map/wave/pallas_call | solution.py:401
  52.5 0.0 copy-start
  52.5 1.9 %copy.17 = f32[24,24,256]{2,1,0:T(8,128)} copy(f32[24,24,256]{2,1,0:T(8,128)} %get-tuple-element.12) | data formatting | bytes 1179648
  54.4 0.0 copy-done
  54.5 0.0 copy-start.1
  54.5 0.6 %copy.18 = f32[64,8]{0,1:T(8,128)} copy(f32[64,8]{0,1:T(8,128)S(1)} %bitcast.3) | data formatting | bytes 4096
  55.0 0.0 copy-done.1
  55.1 0.5 copy.19
Async XLA Ops:
  52.5 1.9 %copy-start = (f32[8,64]{1,0:T(8,128)S(1)}, f32[8,64]{1,0:T(8,128)}, u32[]{:S(2)}) copy-start(f32[8,64]{1,0:T(8,128)} %get-tuple-element.7) | copy-start | bytes 6148
  54.5 0.6 %copy-start.1 = (f32[1,8]{1,0:T(1,128)S(1)}, f32[1,8]{1,0:T(1,128)}, u32[]{:S(2)}) copy-start(f32[1,8]{1,0:T(1,128)} %get-tuple-element.8) | copy-start | bytes 100
where the time goes:
time: 55.7 us; the launch traced here: 55.6 us
  Pallas kernels  51.9 us (93%)
  local copies, waits for them, and re-layouts  3.04 us (5%)
  between operations  0.65 us (1%)
    pallas_call x1, Pallas kernels, per_device(): pl.pallas_call(functools.partial(kernel, ngx, ngy), out_shape=(jax.ShapeD...  51.9 us
    unnamed x7, local copies, waits for them, and re-layouts  3.04 us

commit v1 on v0

--- a/solution.py
+++ b/solution.py
@@ -16,6 +16,10 @@
 damping = 0.6
 radius = 4
 GROUP = 8
+UNROLL = 4
+scale = 0.2
+first_scaled = (4.0, -1.0, 4.0 / 21.0, -1.0 / 56.0)
+second_scaled = (8.0, -1.0, 8.0 / 63.0, -1.0 / 112.0)
 
 
 def split(value):
@@ -50,8 +54,8 @@
     pressure, pressure_old, speed, widths_in, sx_in, sy_in, sz_in, amp_in, rx_in, ry_in, rz_in,
     out, out_traces, out_energy,
     F, SP, LAP, FH, FL, HX, HY, MX, ZX, MY, ZY,
-    BZ, BY, DY, R32, RB, ZM, PS, KX, KY, W, TR, TE, R1, R2,
-    widths, src_x, src_y, src_z, amp, rec_x, rec_y, rec_z, small_sem, load_sem, send_sem, recv_sem, r1_send, r1_recv, r2_send, r2_recv,
+    BZ, BD, R32, RB, ZM, PS, KX, KY, W, TR, TE, R1, R2, LAST, R3,
+    widths, src_x, src_y, src_z, amp, rec_x, rec_y, rec_z, small_sem, load_sem, send_sem, recv_sem, r1_send, r1_recv, r2_send, r2_recv, r3_send, r3_recv,
 ):
     cx, cy, nz = pressure.shape
     nsrc, steps = amp.shape
@@ -77,15 +81,22 @@
     for load in loads + smalls:
         load.start()
 
-    HX[...] = jnp.zeros_like(HX)
     HY[...] = jnp.zeros_like(HY)
 
     barrier = pltpu.get_barrier_semaphore()
-    for o in range(1, ngx):
-        pl.semaphore_signal(barrier, inc=1, device_id={"gx": lax.rem(gx + o, ngx)}, device_id_type=MESH)
-    for o in range(1, ngy):
-        pl.semaphore_signal(barrier, inc=1, device_id={"gy": lax.rem(gy + o, ngy)}, device_id_type=MESH)
-    pl.semaphore_wait(barrier, ngx - 1 + ngy - 1)
+    count = ngx * ngy
+    me = gx * ngy + gy
+
+    def peer(o):
+        p = lax.rem(me + o, count)
+        return p, {"gx": p // ngy, "gy": lax.rem(p, ngy)}
+
+    def greet(o, c):
+        pl.semaphore_signal(barrier, inc=1, device_id=peer(o)[1], device_id_type=MESH)
+        return c
+
+    lax.fori_loop(1, count, greet, 0)
+    pl.semaphore_wait(barrier, count - 1)
 
     def halos(s):
         f = F.at[s]
@@ -138,11 +149,9 @@
     ZX[...] = jnp.zeros_like(ZX)
     MY[...] = jnp.zeros_like(MY)
     ZY[...] = jnp.zeros_like(ZY)
-    TR[...] = jnp.zeros_like(TR)
-    TE[...] = jnp.zeros_like(TE)
 
     z_diff = iota((nz, nz), 0) - iota((nz, nz), 1)
-    BZ[0], BZ[1] = split(by_distance(jnp.abs(z_diff), second_coef, centre_coef))
+    BZ[...] = by_distance(jnp.abs(z_diff), second_scaled, 0.0).astype(BF16)
 
     def block_of(index, size):
         return jnp.floor((index.astype(F32) + 0.5) * (1.0 / size)).astype(jnp.int32)
@@ -150,33 +159,37 @@
     row, col = iota((grows, grows), 0), iota((grows, grows), 1)
     same = block_of(row, cy) == block_of(col, cy)
     diff = col - row
-    BY[0], BY[1] = split(jnp.where(same, by_distance(jnp.abs(diff), second_coef, centre_coef), 0.0))
-    signed = by_distance(jnp.abs(diff), first_coef, 0.0)
-    DY[0], DY[1] = split(jnp.where(same, jnp.where(diff > 0, signed, -signed), 0.0))
+    BD[0:grows] = jnp.where(same, by_distance(jnp.abs(diff), second_scaled, 0.0), 0.0).astype(BF16)
+    signed = by_distance(jnp.abs(diff), first_scaled, 0.0)
+    BD[grows:2 * grows] = jnp.where(same, jnp.where(diff > 0, signed, -signed), 0.0).astype(BF16)
     for load in smalls:
         load.wait()
     w = [widths[i].astype(F32) for i in range(4)]
     KX[...] = profile((iota(KX.shape, 0) + x0).astype(F32), w[0], w[1], count_x)
     KY[...] = profile((iota(KY.shape, 0) + y0).astype(F32), w[2], w[3], count_y)
-    for i in range(cx):
-        W[i] = 1.0 - KX[i, 0:1] * KY[...]
     yy, zz = iota((cy, nz), 0) + y0, iota((cy, nz), 1)
     for s in range(nsrc):
         PS[s] = jnp.where((yy == src_y[s]) & (zz == src_z[s]), 1.0, 0.0)
 
-    cells = iota((1, cx * cy), 1)
-    lanes = iota((1, nz), 1)
-
-    def one_receiver(r, carry):
-        lx, ly = rec_x[r] - x0, rec_y[r] - y0
-        owned = (lx >= 0) & (lx < cx) & (ly >= 0) & (ly < cy)
-        cell = jnp.where(owned, lx * cy + ly, -1)
-        R32[pl.ds(r, 1), :] = jnp.where(cells == cell, 1.0, 0.0)
-        ZM[pl.ds(r, 1), :] = jnp.where(lanes == rec_z[r], 1.0, 0.0)
-        return carry
-
-    lax.fori_loop(0, nrec, one_receiver, 0)
-    RB[...] = R32[...].astype(BF16)
+    def late_setup():
+        for i in range(cx):
+            W[i] = 1.0 - KX[i, 0:1] * KY[...]
+        cells = iota((1, cx * cy), 1)
+        lanes = iota((1, nz), 1)
+
+        def one_receiver(r, carry):
+            lx, ly = rec_x[r] - x0, rec_y[r] - y0
+            owned = (lx >= 0) & (lx < cx) & (ly >= 0) & (ly < cy)
+            cell = jnp.where(owned, lx * cy + ly, -1)
+            R32[pl.ds(r, 1), :] = jnp.where(cells == cell, 1.0, 0.0)
+            ZM[pl.ds(r, 1), :] = jnp.where(lanes == rec_z[r], 1.0, 0.0)
+            return carry
+
+        lax.fori_loop(0, nrec, one_receiver, 0, unroll=4)
+        RB[...] = R32[...].astype(BF16)
+        TR[...] = jnp.zeros_like(TR)
+        TE[...] = jnp.zeros_like(TE)
+
     loads[1].wait()
     loads[2].wait()
 
@@ -191,11 +204,16 @@
         FH[rows, :], FL[rows, :] = fh, fl
         return fh, fl
 
+    def sampled():
+        g = (dot(RB[...], FH[...]) + dot(RB[...], FL[...])) * ZM[...]
+        return jnp.sum(g, axis=1, keepdims=True)
+
+    def total(e):
+        return jnp.sum(jnp.sum(e, axis=0, keepdims=True), axis=1, keepdims=True)
+
     def record(t, e):
-        total = jnp.sum(jnp.sum(e, axis=0, keepdims=True), axis=1, keepdims=True)
-        TE[...] = jnp.where((te_row == t) & (te_lane == nrec), total, TE[...])
-        g = (dot(RB[...], FH[...]) + dot(RB[...], FL[...])) * ZM[...]
-        TR[...] = jnp.where(tr_lane == t, jnp.sum(g, axis=1, keepdims=True), TR[...])
+        TE[...] = jnp.where((te_row == t) & (te_lane == nrec), total(e), TE[...])
+        TR[...] = jnp.where(tr_lane == t, sampled(), TR[...])
 
     p8 = iota((8, nz), 0)
     up, down = [], []
@@ -204,33 +222,54 @@
         up.append(jnp.where(p8 + d < radius, c, 0.0))
         down.append(jnp.where(p8 - d >= radius, c, 0.0))
 
-    def step(t, carry):
+    def gather_copy(axis, buf, send, recv, slot, k, target):
+        return pltpu.make_async_remote_copy(
+            src_ref=TE, dst_ref=buf.at[slot], send_sem=send.at[k], recv_sem=recv.at[slot],
+            device_id={axis: target}, device_id_type=MESH,
+        )
+
+    def gather_start(axis, at, n, buf, send, recv):
+        buf[at] = TE[...]
+        for o in range(1, n):
+            gather_copy(axis, buf, send, recv, at, o, lax.rem(at + o, n)).start()
+
+    def gather_finish(axis, at, n, buf, send, recv):
+        for o in range(1, n):
+            gather_copy(axis, buf, send, recv, lax.rem(at + o, n), o, lax.rem(at + o, n)).wait_recv()
+        for o in range(1, n):
+            gather_copy(axis, buf, send, recv, at, o, lax.rem(at + o, n)).wait_send()
+        v = buf[0]
+        for j in range(1, n):
+            v += buf[j]
+        TE[...] = v
+
+    def step(t, carry, first_step=False):
         s = lax.rem(t, 2)
         o = 1 - s
-
 
         for g in range(groups):
             xs = pl.ds(g * GROUP, GROUP)
             fh, fl = split_group(s, g)
-            sz = dot(fh, BZ[0]) + dot(fl, BZ[0]) + dot(fh, BZ[1])
-            sy = dot(BY[0], fh) + dot(BY[0], fl) + dot(BY[1], fh)
+            sz = dot(fh, BZ[...]) + dot(fl, BZ[...])
 
             @pl.when(jnp.logical_not(edge_y))
             def _():
-                LAP[xs] = (sz + sy).reshape(GROUP, cy, nz)
+                sy = dot(BD[0:grows], fh) + dot(BD[0:grows], fl)
+                LAP[xs] = (scale * (sz + sy)).reshape(GROUP, cy, nz)
 
             @pl.when(edge_y)
             def _():
                 ky = KY[...][None]
                 ty = ky - 1.0
+                both = dot(BD[...], fh) + dot(BD[...], fl)
                 mh, ml = split(MY[xs].reshape(grows, nz))
-                dm = dot(DY[0], mh) + dot(DY[0], ml) + dot(DY[1], mh)
-                bend = (sy + dm).reshape(GROUP, cy, nz)
+                dm = dot(BD[grows:2 * grows], mh) + dot(BD[grows:2 * grows], ml)
+                f = F[s, pl.ds(radius + g * GROUP, GROUP)]
+                bend = centre_coef * f + (scale * (both[0:grows] + dm)).reshape(GROUP, cy, nz)
                 zy = ky * ZY[xs] + ty * bend
                 ZY[xs] = zy
-                LAP[xs] = sz.reshape(GROUP, cy, nz) + bend + zy
-                df = dot(DY[0], fh) + dot(DY[0], fl) + dot(DY[1], fh)
-                MY[xs] = ky * MY[xs] + ty * df.reshape(GROUP, cy, nz)
+                LAP[xs] = (scale * sz).reshape(GROUP, cy, nz) + (bend - centre_coef * f) + zy
+                MY[xs] = ky * MY[xs] + (ty * scale) * both[grows:2 * grows].reshape(GROUP, cy, nz)
 
         def second_x(i):
             v = centre_coef * F[s, radius + i]
@@ -256,14 +295,16 @@
                 ZX[i] = zx
                 lap += zx
                 MX[o, radius + i] = kx * MX[s, radius + i] + tx * first(F, i)
-            v = 2.0 * f - F[o, radius + i] + SP[i] * (lap + bend)
+            v = 2.0 * f - F[o, radius + i] + SP[i] * (lap + bend + (2.0 * centre_coef) * f)
             for q in range(nsrc):
                 v += jnp.where(src_x[q] - x0 == i, amp[q, t], 0.0) * PS[q]
             F[o, radius + i] = v
-            return e + W[i] * (f * f)
+            return e if first_step else e + W[i] * (f * f)
 
         def finish(edge):
-            record(t - 1, lax.fori_loop(0, cx, functools.partial(update, edge), jnp.zeros((cy, nz), F32)))
+            e = lax.fori_loop(0, cx, functools.partial(update, edge), jnp.zeros((cy, nz), F32), unroll=UNROLL)
+            if not first_step:
+                record(t - 1, e)
 
         @pl.when(edge_x)
         def _():
@@ -272,6 +313,15 @@
         @pl.when(jnp.logical_not(edge_x))
         def _():
             finish(False)
+
+        if first_step:
+            late_setup()
+        else:
+            @pl.when(t == steps - 1)
+            def _():
+                flat = jnp.transpose(TR[...])[0:steps]
+                TE[...] += jnp.concatenate([flat, jnp.zeros((steps, TE.shape[1] - nrec), F32)], axis=1)
+                gather_start("gx", gx, ngx, R1, r1_send, r1_recv)
 
         now, later = halos(s), halos(o)
         more = t < steps - 1
@@ -341,10 +391,9 @@
         resend(3)
         return carry
 
-    lax.fori_loop(0, steps, step, 0)
+    step(0, 0, True)
+    lax.fori_loop(1, steps, step, 0)
     last = steps % 2
-    store = pltpu.make_async_copy(F.at[last, pl.ds(radius, cx)], out, load_sem.at[0])
-    store.start()
     for g in range(groups):
         split_group(last, g)
 
@@ -352,40 +401,51 @@
         f = F[last, radius + i]
         return e + W[i] * (f * f)
 
-    record(steps - 1, lax.fori_loop(0, cx, energy_row, jnp.zeros((cy, nz), F32)))
-    flat = jnp.transpose(TR[...])[0:steps]
-    TE[...] += jnp.concatenate([flat, jnp.zeros((steps, TE.shape[1] - nrec), F32)], axis=1)
-
-    def reduce_over(axis, me, n, buf, send, recv):
-        buf[me] = TE[...]
-
-        def copy(slot, k, target):
-            return pltpu.make_async_remote_copy(
-                src_ref=TE, dst_ref=buf.at[slot], send_sem=send.at[k], recv_sem=recv.at[slot],
-                device_id={axis: target}, device_id_type=MESH,
-            )
-
-        for o in range(1, n):
-            copy(me, o, lax.rem(me + o, n)).start()
-        for o in range(1, n):
-            copy(lax.rem(me + o, n), o, lax.rem(me + o, n)).wait_recv()
-        for o in range(1, n):
-            copy(me, o, lax.rem(me + o, n)).wait_send()
-        v = buf[0]
-        for j in range(1, n):
-            v += buf[j]
-        TE[...] = v
-
-    reduce_over("gx", gx, ngx, R1, r1_send, r1_recv)
-    reduce_over("gy", gy, ngy, R2, r2_send, r2_recv)
-
+    amount = total(lax.fori_loop(0, cx, energy_row, jnp.zeros((cy, nz), F32), unroll=UNROLL))
+    row = jnp.transpose(jnp.broadcast_to(sampled(), TR.shape))[0:1]
+    row = jnp.concatenate([row, jnp.zeros((1, TE.shape[1] - nrec), F32)], axis=1)
+    LAST[0] = jnp.where(iota(row.shape, 1) == nrec, amount, row)
+    R3[me] = LAST[0]
+
+    def last_copy(slot, o, target):
+        return pltpu.make_async_remote_copy(
+            src_ref=LAST, dst_ref=R3.at[pl.ds(slot, 1)], send_sem=r3_send.at[o], recv_sem=r3_recv.at[slot],
+            device_id=target, device_id_type=MESH,
+        )
+
+    def last_start(o, c):
+        last_copy(me, o, peer(o)[1]).start()
+        return c
+
+    def last_wait(o, c):
+        p, target = peer(o)
+        last_copy(p, o, target).wait_recv()
+        last_copy(me, o, target).wait_send()
+        return c
+
+    lax.fori_loop(1, count, last_start, 0)
+    out[...] = F[last, pl.ds(radius, cx)]
+    gather_finish("gx", gx, ngx, R1, r1_send, r1_recv)
+    gather_start("gy", gy, ngy, R2, r2_send, r2_recv)
     def total_of(count, low, high):
         return jnp.sum(profile(iota((1, count), 1).astype(F32), low, high, count), axis=1, keepdims=True)
 
     norm = nz * (float(count_x * count_y) - total_of(count_x, w[0], w[1]) * total_of(count_y, w[2], w[3]))
+    gather_finish("gy", gy, ngy, R2, r2_send, r2_recv)
+    lax.fori_loop(1, count, last_wait, 0)
+    final = jnp.sum(R3[...], axis=0)
+    TE[...] = jnp.where(te_row == steps - 1, final, TE[...])
     out_traces[...] = TE[:, 0:nrec]
     out_energy[...] = jnp.transpose(TE[...])[nrec:nrec + 1] / norm
-    store.wait()
+
+
+def store(*refs):
+    sem = refs[-1]
+    copies = [pltpu.make_async_copy(refs[n], refs[n + 3], sem.at[n]) for n in range(3)]
+    for copy in copies:
+        copy.start()
+    for copy in copies:
+        copy.wait()
 
 
 def solution(mesh):
@@ -398,19 +458,12 @@
         lanes = (nrec // 128 + 1) * 128
         vmem = functools.partial(pltpu.VMEM)
         grows = GROUP * cy
-        final, traces, energy = pl.pallas_call(
+        shapes = ((cx, cy, nz), (steps, nrec), (1, steps))
+        held = pl.pallas_call(
             functools.partial(kernel, ngx, ngy),
-            out_shape=(
-                jax.ShapeDtypeStruct((cx, cy, nz), F32),
-                jax.ShapeDtypeStruct((steps, nrec), F32),
-                jax.ShapeDtypeStruct((1, steps), F32),
-            ),
+            out_shape=tuple(vmem(shape, F32) for shape in shapes),
             in_specs=[pl.BlockSpec(memory_space=pltpu.HBM)] * 11,
-            out_specs=(
-                pl.BlockSpec(memory_space=pl.ANY),
-                pl.BlockSpec(memory_space=pltpu.VMEM),
-                pl.BlockSpec(memory_space=pltpu.VMEM),
-            ),
+            out_specs=(pl.BlockSpec(memory_space=pltpu.VMEM),) * 3,
             scratch_shapes=[
                 vmem((2, cx + 2 * radius, cy, nz), F32),
                 vmem((cx, cy, nz), F32),
@@ -423,9 +476,8 @@
                 vmem((cx, cy, nz), F32),
                 vmem((cx, cy, nz), F32),
                 vmem((cx, cy, nz), F32),
-                vmem((2, nz, nz), BF16),
-                vmem((2, grows, grows), BF16),
-                vmem((2, grows, grows), BF16),
+                vmem((nz, nz), BF16),
+                vmem((2 * grows, grows), BF16),
                 vmem((nrec, cx * cy), F32),
                 vmem((nrec, cx * cy), BF16),
                 vmem((nrec, nz), F32),
@@ -437,6 +489,8 @@
                 vmem((steps, lanes), F32),
                 vmem((ngx, steps, lanes), F32),
                 vmem((ngy, steps, lanes), F32),
+                vmem((1, 1, lanes), F32),
+                vmem((ngx * ngy, 1, lanes), F32),
                 pltpu.SMEM(widths.shape, jnp.int32),
                 pltpu.SMEM(sx.shape, jnp.int32),
                 pltpu.SMEM(sy.shape, jnp.int32),
@@ -453,12 +507,23 @@
                 pltpu.SemaphoreType.DMA((ngx,)),
                 pltpu.SemaphoreType.DMA((ngy,)),
                 pltpu.SemaphoreType.DMA((ngy,)),
+                pltpu.SemaphoreType.DMA((ngx * ngy,)),
+                pltpu.SemaphoreType.DMA((ngx * ngy,)),
             ],
             compiler_params=pltpu.CompilerParams(
-                collective_id=0, has_side_effects=True, vmem_limit_bytes=67043328
+                collective_id=0, has_side_effects=True, vmem_limit_bytes=64 * 1024 * 1024 - 2 * 1024 * 1024
             ),
             name="wave",
         )(pressure, pressure_old, speed, widths, sx, sy, sz, amp.T, rx, ry, rz)
+        final, traces, energy = pl.pallas_call(
+            store,
+            out_shape=tuple(jax.ShapeDtypeStruct(shape, F32) for shape in shapes),
+            in_specs=[pl.BlockSpec(memory_space=pltpu.VMEM)] * 3,
+            out_specs=(pl.BlockSpec(memory_space=pltpu.HBM),) * 3,
+            scratch_shapes=[pltpu.SemaphoreType.DMA((3,))],
+            compiler_params=pltpu.CompilerParams(has_side_effects=True, vmem_limit_bytes=1024 * 1024),
+            name="store",
+        )(*held)
         return final, traces.T, energy.reshape(steps)
 
     in_specs = (P("gx", "gy", None),) * 3 + (P(),) * 8

time: 55.7 us -> 52.7 us (0.946)
  local copies, waits for them, and re-layouts: 3.04 us -> 0 us
    unnamed x7 -> x0, local copies, waits for them, and re-layouts: 3.04 us -> none
    pallas_call x1 -> x2, Pallas kernels: 51.9 us -> 51.9 us  [the longest x1 51 us: per_device(): pl.pallas_call(functools.partial(kernel, ngx, ngy), out_shape=tuple((vmem...]
where the time goes in v1:
time: 52.7 us; the launch traced here: 52.5 us
  Pallas kernels  51.9 us (98%)
  between operations  0.64 us (1%)
    pallas_call x1, Pallas kernels, per_device(): pl.pallas_call(functools.partial(kernel, ngx, ngy), out_shape=tuple((vmem...  51 us

profile of v1, /device:TPU:0, one launch (start us, length us, event | category | flops | bytes accessed | tf_op | source)
XLA Modules:
  0.0 52.5 jit_solution(16206181728866363501)
XLA Ops:
  0.6 51.0 %wave.1 = (f32[24,24,256]{2,1,0:T(8,128)S(1)}, f32[8,64]{1,0:T(8,128)S(1)}, f32[1,8]{1,0:T(1,128)S(1)}) custom-call(f32[24,24,256]{2,1,0:T(8,128)} %pressure.1, f32[24,24,256]{2,1,0:T(8,128)} %pressure_old.1, f32[24,24,256]{2,1,0:T(8,128)} %speed.1, s32[4]{0:T(128)} %widths_in.1, s32[4]{0:T(128)} %sx_in.1, s32[4]{0:T(128)} %sy_in.1, s32[4]{0:T(128)} %sz_in.1, ...), custom_call_target="tpu_custom_call" | custom-call | tf_op jit(solution)/shard_map/wave/pallas_call | solution.py:462
  51.7 0.8 %store.1 = (f32[24,24,256]{2,1,0:T(8,128)}, f32[8,64]{1,0:T(8,128)}, f32[1,8]{1,0:T(1,128)}) custom-call(f32[24,24,256]{2,1,0:T(8,128)S(1)} %get-tuple-element.9.refs_0_, f32[8,64]{1,0:T(8,128)S(1)} %get-tuple-element.10.refs_1_, f32[1,8]{1,0:T(1,128)S(1)} %get-tuple-element.11.refs_2_), custom_call_target="tpu_custom_call" | custom-call | tf_op jit(solution)/shard_map/store/pallas_call | solution.py:518

commit v2 on v1

--- a/solution.py
+++ b/solution.py
@@ -10,14 +10,13 @@
 MESH = pl.DeviceIdType.MESH
 F32 = jnp.float32
 BF16 = jnp.bfloat16
-first_coef = (0.8, -0.2, 4.0 / 105.0, -1.0 / 280.0)
-second_coef = (1.6, -0.2, 8.0 / 315.0, -1.0 / 560.0)
 centre_coef = -205.0 / 72.0
 damping = 0.6
 radius = 4
 GROUP = 8
 UNROLL = 4
 scale = 0.2
+centre_scaled = centre_coef / scale
 first_scaled = (4.0, -1.0, 4.0 / 21.0, -1.0 / 56.0)
 second_scaled = (8.0, -1.0, 8.0 / 63.0, -1.0 / 112.0)
 
@@ -53,9 +52,9 @@
     ngx, ngy,
     pressure, pressure_old, speed, widths_in, sx_in, sy_in, sz_in, amp_in, rx_in, ry_in, rz_in,
     out, out_traces, out_energy,
-    F, SP, LAP, FH, FL, HX, HY, MX, ZX, MY, ZY,
+    F, SP, AF, LAP, FH, FL, HX, HY, MX, ZX, MY, ZY,
     BZ, BD, R32, RB, ZM, PS, KX, KY, W, TR, TE, R1, R2, LAST, R3,
-    widths, src_x, src_y, src_z, amp, rec_x, rec_y, rec_z, small_sem, load_sem, send_sem, recv_sem, r1_send, r1_recv, r2_send, r2_recv, r3_send, r3_recv,
+    widths, src_x, src_y, src_z, amp, rec_x, rec_y, rec_z, small_sem, load_sem, x_send, x_recv, y_send, y_recv, r1_send, r1_recv, r2_send, r2_recv, r3_send, r3_recv,
 ):
     cx, cy, nz = pressure.shape
     nsrc, steps = amp.shape
@@ -91,53 +90,61 @@
         p = lax.rem(me + o, count)
         return p, {"gx": p // ngy, "gy": lax.rem(p, ngy)}
 
-    def greet(o, c):
-        pl.semaphore_signal(barrier, inc=1, device_id=peer(o)[1], device_id_type=MESH)
-        return c
-
-    lax.fori_loop(1, count, greet, 0)
-    pl.semaphore_wait(barrier, count - 1)
-
-    def halos(s):
-        f = F.at[s]
-
-        def send(k, src, dst, target):
-            return pltpu.make_async_remote_copy(
-                src_ref=src, dst_ref=dst, send_sem=send_sem.at[k], recv_sem=recv_sem.at[s, k],
-                device_id=target, device_id_type=MESH,
-            )
-
-        return (
-            (gx < ngx - 1, gx > 0, send(0, f.at[pl.ds(cx, radius)], HX.at[s, 0], {"gx": gx + 1})),
-            (gx > 0, gx < ngx - 1, send(1, f.at[pl.ds(radius, radius)], HX.at[s, 1], {"gx": gx - 1})),
-            (gy < ngy - 1, gy > 0, send(2, f.at[pl.ds(radius, cx), pl.ds(cy - radius, radius)],
-                                        HY.at[s, :, pl.ds(0, radius)], {"gy": gy + 1})),
-            (gy > 0, gy < ngy - 1, send(3, f.at[pl.ds(radius, cx), pl.ds(0, radius)],
-                                        HY.at[s, :, pl.ds(radius, radius)], {"gy": gy - 1})),
+    near = ((gx > 0, {"gx": gx - 1}), (gx < ngx - 1, {"gx": gx + 1}), (gy > 0, {"gy": gy - 1}), (gy < ngy - 1, {"gy": gy + 1}))
+    for there, who in near:
+        @pl.when(there)
+        def _(who=who):
+            pl.semaphore_signal(barrier, inc=1, device_id=who, device_id_type=MESH)
+    pl.semaphore_wait(barrier, sum(there.astype(jnp.int32) for there, _ in near))
+
+    odd = lax.rem(gx, 2)
+    pieces = cy // 8
+    here_x = lambda side: jnp.where(side == 1, gx < ngx - 1, gx > 0)
+    to_y = (gy < ngy - 1, gy > 0)
+    from_y = (gy > 0, gy < ngy - 1)
+
+    def x_copy(slot, side, c, arriving):
+        rows = pl.ds(8 * c, 8)
+        at = side if arriving else 1 - side
+        return pltpu.make_async_remote_copy(
+            src_ref=F.at[slot, pl.ds(radius + side * (cx - radius), radius), rows],
+            dst_ref=HX.at[slot, at, :, rows],
+            send_sem=x_send.at[side * pieces + c], recv_sem=x_recv.at[slot, at * pieces + c],
+            device_id={"gx": gx + 2 * side - 1}, device_id_type=MESH,
         )
 
-    upper_first = lax.rem(gx, 2) == 1
-
-    def start_sends(s):
-        h = halos(s)
-
-        def go(k):
-            @pl.when(h[k][0])
+    def y_copy(slot, d, part, first, count_planes):
+        return pltpu.make_async_remote_copy(
+            src_ref=F.at[slot, pl.ds(radius + first, count_planes), pl.ds(0 if d else cy - radius, radius)],
+            dst_ref=HY.at[slot, pl.ds(first, count_planes), pl.ds(radius if d else 0, radius)],
+            send_sem=y_send.at[2 * part + d], recv_sem=y_recv.at[slot, 2 * part + d],
+            device_id={"gy": gy - 1 if d else gy + 1}, device_id_type=MESH,
+        )
+
+    middle = (2, radius, cx - 2 * radius)
+
+    def edge_part(side):
+        return (side, side * (cx - radius), radius)
+
+    def start_sends(slot):
+        def one_side(n, c):
+            side = lax.rem(n + odd, 2)
+
+            @pl.when(here_x(side))
             def _():
-                h[k][2].start()
-
-        @pl.when(upper_first)
-        def _():
-            go(0)
-            go(1)
-
-        @pl.when(jnp.logical_not(upper_first))
-        def _():
-            go(1)
-            go(0)
-
-        go(2)
-        go(3)
+                for p in range(pieces):
+                    x_copy(slot, side, p, False).start()
+            for d in range(2):
+                @pl.when(to_y[d])
+                def _(d=d):
+                    y_copy(slot, d, *edge_part(side)).start()
+            return c
+
+        lax.fori_loop(0, 2, one_side, 0)
+        for d in range(2):
+            @pl.when(to_y[d])
+            def _(d=d):
+                y_copy(slot, d, *middle).start()
 
     loads[0].wait()
     start_sends(0)
@@ -193,6 +200,13 @@
     loads[1].wait()
     loads[2].wait()
 
+    def prescale(i, c):
+        v = SP[i]
+        AF[i] = 2.0 + (3.0 * centre_coef) * v
+        SP[i] = scale * v
+        return c
+
+    lax.fori_loop(0, cx, prescale, 0, unroll=4)
     edge_x = (gx == 0) | (gx == ngx - 1)
     edge_y = (gy == 0) | (gy == ngy - 1)
     te_row, te_lane = iota(TE.shape, 0), iota(TE.shape, 1)
@@ -218,7 +232,7 @@
     p8 = iota((8, nz), 0)
     up, down = [], []
     for d in range(radius):
-        c = second_coef[radius - 1 - d]
+        c = second_scaled[radius - 1 - d]
         up.append(jnp.where(p8 + d < radius, c, 0.0))
         down.append(jnp.where(p8 - d >= radius, c, 0.0))
 
@@ -247,41 +261,38 @@
         s = lax.rem(t, 2)
         o = 1 - s
 
-        for g in range(groups):
-            xs = pl.ds(g * GROUP, GROUP)
-            fh, fl = split_group(s, g)
-            sz = dot(fh, BZ[...]) + dot(fl, BZ[...])
-
-            @pl.when(jnp.logical_not(edge_y))
-            def _():
+        @pl.when(jnp.logical_not(edge_y))
+        def _():
+            for g in range(groups):
+                fh, fl = split_group(s, g)
+                sums = dot(fh, BZ[...]) + dot(fl, BZ[...]) + dot(BD[0:grows], fh) + dot(BD[0:grows], fl)
+                LAP[pl.ds(g * GROUP, GROUP)] = sums.reshape(GROUP, cy, nz)
+
+        @pl.when(edge_y)
+        def _():
+            ky = KY[...][None]
+            ty = ky - 1.0
+            for g in range(groups):
+                xs = pl.ds(g * GROUP, GROUP)
+                fh, fl = split_group(s, g)
+                sz = dot(fh, BZ[...]) + dot(fl, BZ[...])
                 sy = dot(BD[0:grows], fh) + dot(BD[0:grows], fl)
-                LAP[xs] = (scale * (sz + sy)).reshape(GROUP, cy, nz)
-
-            @pl.when(edge_y)
-            def _():
-                ky = KY[...][None]
-                ty = ky - 1.0
-                both = dot(BD[...], fh) + dot(BD[...], fl)
                 mh, ml = split(MY[xs].reshape(grows, nz))
-                dm = dot(BD[grows:2 * grows], mh) + dot(BD[grows:2 * grows], ml)
+                bend = (sy + dot(BD[grows:2 * grows], mh) + dot(BD[grows:2 * grows], ml)).reshape(GROUP, cy, nz)
+                df = dot(BD[grows:2 * grows], fh) + dot(BD[grows:2 * grows], fl)
                 f = F[s, pl.ds(radius + g * GROUP, GROUP)]
-                bend = centre_coef * f + (scale * (both[0:grows] + dm)).reshape(GROUP, cy, nz)
-                zy = ky * ZY[xs] + ty * bend
+                zy = ky * ZY[xs] + ty * (bend + centre_scaled * f)
                 ZY[xs] = zy
-                LAP[xs] = (scale * sz).reshape(GROUP, cy, nz) + (bend - centre_coef * f) + zy
-                MY[xs] = ky * MY[xs] + (ty * scale) * both[grows:2 * grows].reshape(GROUP, cy, nz)
+                LAP[xs] = sz.reshape(GROUP, cy, nz) + bend + zy
+                MY[xs] = ky * MY[xs] + (scale * ty) * df.reshape(GROUP, cy, nz)
 
         def second_x(i):
-            v = centre_coef * F[s, radius + i]
-            for k in range(1, 5):
-                v += second_coef[k - 1] * (F[s, radius + i + k] + F[s, radius + i - k])
-            return v
+            pair = [F[s, radius + i + k] + F[s, radius + i - k] for k in range(1, 5)]
+            return second_scaled[0] * pair[0] - pair[1] + second_scaled[2] * pair[2] + second_scaled[3] * pair[3]
 
         def first(ref, i):
-            v = first_coef[0] * (ref[s, radius + i + 1] - ref[s, radius + i - 1])
-            for k in range(2, 5):
-                v += first_coef[k - 1] * (ref[s, radius + i + k] - ref[s, radius + i - k])
-            return v
+            pair = [ref[s, radius + i + k] - ref[s, radius + i - k] for k in range(1, 5)]
+            return first_scaled[0] * pair[0] - pair[1] + first_scaled[2] * pair[2] + first_scaled[3] * pair[3]
 
         def update(edge, i, e):
             f = F[s, radius + i]
@@ -291,11 +302,11 @@
                 kx = KX[i, 0:1]
                 tx = kx - 1.0
                 bend += first(MX, i)
-                zx = kx * ZX[i] + tx * bend
+                zx = kx * ZX[i] + tx * (bend + centre_scaled * f)
                 ZX[i] = zx
                 lap += zx
-                MX[o, radius + i] = kx * MX[s, radius + i] + tx * first(F, i)
-            v = 2.0 * f - F[o, radius + i] + SP[i] * (lap + bend + (2.0 * centre_coef) * f)
+                MX[o, radius + i] = kx * MX[s, radius + i] + (scale * tx) * first(F, i)
+            v = AF[i] * f - F[o, radius + i] + SP[i] * (lap + bend)
             for q in range(nsrc):
                 v += jnp.where(src_x[q] - x0 == i, amp[q, t], 0.0) * PS[q]
             F[o, radius + i] = v
@@ -323,77 +334,73 @@
                 TE[...] += jnp.concatenate([flat, jnp.zeros((steps, TE.shape[1] - nrec), F32)], axis=1)
                 gather_start("gx", gx, ngx, R1, r1_send, r1_recv)
 
-        now, later = halos(s), halos(o)
         more = t < steps - 1
 
-        def received(k):
-            @pl.when(now[k][1])
+        def halo_y(part):
+            _, begin, n = part
+            for d in range(2):
+                @pl.when(from_y[d])
+                def _(d=d):
+                    y_copy(s, d, *part).wait_recv()
+
+            def one(k, c):
+                i = begin + k
+                h = HY[s, i]
+                v = (up[0] + down[0]) * h
+                for d in range(1, radius):
+                    v += up[d] * pltpu.roll(h, 8 - d, 0) + down[d] * pltpu.roll(h, d, 0)
+                F[o, radius + i, 0:8] += SP[i, 0:8] * jnp.where(p8 < radius, v, 0.0)
+                F[o, radius + i, cy - 8:cy] += SP[i, cy - 8:cy] * jnp.where(p8 < radius, 0.0, v)
+                return c
+
+            lax.fori_loop(0, n, one, 0, unroll=4)
+
+        def send_y(part):
+            for d in range(2):
+                @pl.when(to_y[d])
+                def _(d=d):
+                    y_copy(s, d, *part).wait_send()
+
+                @pl.when(to_y[d] & more)
+                def _(d=d):
+                    y_copy(o, d, *part).start()
+
+        halo_y(middle)
+        send_y(middle)
+
+        def one_side(n, carry):
+            side = lax.rem(n + odd, 2)
+            part = edge_part(side)
+            halo_y(part)
+
+            @pl.when(here_x(side))
             def _():
-                now[k][2].wait_recv()
-
-        def resend(k):
-            @pl.when(now[k][0])
-            def _():
-                now[k][2].wait_send()
-
-            @pl.when(now[k][0] & more)
-            def _():
-                later[k][2].start()
-
-        received(2)
-        received(3)
-
-        def halo_y(i, c):
-            h = HY[s, i]
-            v = (up[0] + down[0]) * h
-            for d in range(1, radius):
-                v += up[d] * pltpu.roll(h, 8 - d, 0) + down[d] * pltpu.roll(h, d, 0)
-            F[o, radius + i, 0:8] += SP[i, 0:8] * jnp.where(p8 < radius, v, 0.0)
-            F[o, radius + i, cy - 8:cy] += SP[i, cy - 8:cy] * jnp.where(p8 < radius, 0.0, v)
-            return c
-
-        lax.fori_loop(0, cx, halo_y, 0, unroll=4)
-
-        def low_side():
-            @pl.when(gx > 0)
-            def _():
-                now[0][2].wait_recv()
-                for j in range(radius):
-                    v = second_coef[j] * HX[s, 0, radius - 1]
-                    for k in range(j + 2, 5):
-                        v += second_coef[k - 1] * HX[s, 0, radius + j - k]
-                    F[o, radius + j] += SP[j] * v
-            resend(1)
-
-        def high_side():
-            @pl.when(gx < ngx - 1)
-            def _():
-                now[1][2].wait_recv()
-                for j in range(radius):
-                    i = cx - 1 - j
-                    v = second_coef[j] * HX[s, 1, 0]
-                    for k in range(j + 2, 5):
-                        v += second_coef[k - 1] * HX[s, 1, k - 1 - j]
-                    F[o, radius + i] += SP[i] * v
-            resend(0)
-
-        @pl.when(upper_first)
-        def _():
-            high_side()
-            low_side()
-
-        @pl.when(jnp.logical_not(upper_first))
-        def _():
-            low_side()
-            high_side()
-
-        resend(2)
-        resend(3)
+                for p in range(pieces):
+                    rows = pl.ds(8 * p, 8)
+                    x_copy(s, side, p, True).wait_recv()
+                    h = [HX[s, side, jnp.where(side == 1, m, radius - 1 - m), rows] for m in range(radius)]
+                    for j in range(radius):
+                        i = jnp.where(side == 1, cx - 1 - j, j)
+                        v = second_scaled[j] * h[0]
+                        for k in range(j + 2, 5):
+                            v += second_scaled[k - 1] * h[k - 1 - j]
+                        F[o, radius + i, rows] += SP[i, rows] * v
+                    x_copy(s, side, p, False).wait_send()
+
+                    @pl.when(more)
+                    def _():
+                        x_copy(o, side, p, False).start()
+
+            send_y(part)
+            return carry
+
+        lax.fori_loop(0, 2, one_side, 0)
         return carry
 
     step(0, 0, True)
     lax.fori_loop(1, steps, step, 0)
     last = steps % 2
+    gather_finish("gx", gx, ngx, R1, r1_send, r1_recv)
     for g in range(groups):
         split_group(last, g)
 
@@ -425,7 +432,6 @@
 
     lax.fori_loop(1, count, last_start, 0)
     out[...] = F[last, pl.ds(radius, cx)]
-    gather_finish("gx", gx, ngx, R1, r1_send, r1_recv)
     gather_start("gy", gy, ngy, R2, r2_send, r2_recv)
     def total_of(count, low, high):
         return jnp.sum(profile(iota((1, count), 1).astype(F32), low, high, count), axis=1, keepdims=True)
@@ -466,6 +472,7 @@
             out_specs=(pl.BlockSpec(memory_space=pltpu.VMEM),) * 3,
             scratch_shapes=[
                 vmem((2, cx + 2 * radius, cy, nz), F32),
+                vmem((cx, cy, nz), F32),
                 vmem((cx, cy, nz), F32),
                 vmem((cx, cy, nz), F32),
                 vmem((cx * cy, nz), BF16),
@@ -501,8 +508,10 @@
                 pltpu.SMEM(rz.shape, jnp.int32),
                 pltpu.SemaphoreType.DMA((8,)),
                 pltpu.SemaphoreType.DMA((3,)),
-                pltpu.SemaphoreType.DMA((4,)),
-                pltpu.SemaphoreType.DMA((2, 4)),
+                pltpu.SemaphoreType.DMA((2 * (cy // 8),)),
+                pltpu.SemaphoreType.DMA((2, 2 * (cy // 8))),
+                pltpu.SemaphoreType.DMA((6,)),
+                pltpu.SemaphoreType.DMA((2, 6)),
                 pltpu.SemaphoreType.DMA((ngx,)),
                 pltpu.SemaphoreType.DMA((ngx,)),
                 pltpu.SemaphoreType.DMA((ngy,)),

time: 52.7 us -> 50.5 us (0.958)
  Pallas kernels: 51.9 us -> 49.8 us
    pallas_call x1, Pallas kernels: 51 us -> 48.9 us  [per_device(): pl.pallas_call(functools.partial(kernel, ngx, ngy), out_shape=tuple((vmem...]
where the time goes in v2:
time: 50.5 us; the launch traced here: 50.4 us
  Pallas kernels  49.8 us (99%)
  between operations  0.64 us (1%)
    pallas_call x1, Pallas kernels, per_device(): pl.pallas_call(functools.partial(kernel, ngx, ngy), out_shape=tuple((vmem...  48.9 us

profile of v2, /device:TPU:0, one launch (start us, length us, event | category | flops | bytes accessed | tf_op | source)
XLA Modules:
  0.0 50.4 jit_solution(4652354248267927454)
XLA Ops:
  0.6 48.9 %wave.1 = (f32[24,24,256]{2,1,0:T(8,128)S(1)}, f32[8,64]{1,0:T(8,128)S(1)}, f32[1,8]{1,0:T(1,128)S(1)}) custom-call(f32[24,24,256]{2,1,0:T(8,128)} %pressure.1, f32[24,24,256]{2,1,0:T(8,128)} %pressure_old.1, f32[24,24,256]{2,1,0:T(8,128)} %speed.1, s32[4]{0:T(128)} %widths_in.1, s32[4]{0:T(128)} %sx_in.1, s32[4]{0:T(128)} %sy_in.1, s32[4]{0:T(128)} %sz_in.1, ...), custom_call_target="tpu_custom_call" | custom-call | tf_op jit(solution)/shard_map/wave/pallas_call | solution.py:468
  49.5 0.8 %store.1 = (f32[24,24,256]{2,1,0:T(8,128)}, f32[8,64]{1,0:T(8,128)}, f32[1,8]{1,0:T(1,128)}) custom-call(f32[24,24,256]{2,1,0:T(8,128)S(1)} %get-tuple-element.9.refs_0_, f32[8,64]{1,0:T(8,128)S(1)} %get-tuple-element.10.refs_1_, f32[1,8]{1,0:T(1,128)S(1)} %get-tuple-element.11.refs_2_), custom_call_target="tpu_custom_call" | custom-call | tf_op jit(solution)/shard_map/store/pallas_call | solution.py:527
